TPU v7x, 32 devices: a whole 2x2x4 slice. The times are simulated.
32 devices in a mesh: batch: 8 (over z, core), vocab: 4 (over y, x).
Axes of the slice: x: 2, y: 2, z: 4, core: 2. Of those that a mesh axis runs over, the one named last changes fastest.
Arguments:
- window_ids: int32 [3, 16, 8], P(None, 'batch'), may hold values from 0 to 16383
- pool_ids: int32 [3, 16, 8], P(None, 'batch'), may hold values from 0 to 16383
- accepted: int32 [2, 16], P(None, 'batch'), may hold values from 1 to 8
- converged: int32 [2, 16], P(None, 'batch'), may hold values 0 or 1
- cache_lens: int32 [16], P('batch'), may hold values from 1 to 128
- table: bfloat16 [16384, 4608], P(('batch', 'vocab')), may hold values from -0.29882812 to 0.29882812
- attn_gain: float32 [4608], replicated, may hold values from 0.25 to 1.75
- post_gain: float32 [4608], replicated, may hold values from 0.25 to 1.75
- final_gain: float32 [4608], replicated, may hold values from 0.25 to 1.75
- w_query: bfloat16 [4608, 1024], P(None, 'vocab'), may hold values from -0.09375 to 0.09375
- w_key: bfloat16 [4608, 512], P(None, 'vocab'), may hold values from -0.09375 to 0.09375
- w_value: bfloat16 [4608, 512], P(None, 'vocab'), may hold values from -0.09375 to 0.09375
- w_out: bfloat16 [1024, 4608], P('vocab'), may hold values from -0.1875 to 0.1875
- cache_keys: bfloat16 [16, 4, 128, 128], P('batch', 'vocab'), may hold values from -6 to 6
- cache_values: bfloat16 [16, 4, 128, 128], P('batch', 'vocab'), may hold values from -6 to 6
Outputs:
- log_total: float32 [3, 16, 8], P(None, 'batch')
- best_logit: float32 [3, 16, 8], P(None, 'batch')
- pool_score: float32 [3, 16, 8], P(None, 'batch')
Inputs may be any that keep to these rules, and one draw needn't show every extreme that they name: `converged`: 1 marks a window at its fixed point, whose tokens are all accepted.
All inputs are finite; a program needn't handle non-finite values. No bound on the sum of `converged` on one device may be relied on, other than what follows from the above.
Results may differ from a plain program's by a relative error of at most 0.00036.
Values may be sent and summed in bfloat16 or wider, within the bound.
No kernel may reach another device: no remote copies, remote signals or barrier semaphores. Data moves between devices by JAX's collectives and lax.ppermute only.
A program may use at most 128 MiB of HBM per device.

v0:
```python
import math
import jax
import jax.numpy as jnp
from jax import lax
from jax.sharding import PartitionSpec as P

epsilon = 1e-06
query_scalar = 144.0
score_cap = 50.0
logit_cap = 30.0


def normalize(values_in, gain):
    return (
        values_in
        * lax.rsqrt(jnp.mean(values_in * values_in, axis=-1, keepdims=True) + epsilon)
        * gain
    )


def rotate(values_in, positions):
    half_size = values_in.shape[-1] // 2
    freqs = 10000.0 ** (-jnp.arange(half_size, dtype=jnp.float32) / half_size)
    angles = positions.astype(jnp.float32)[..., None] * freqs
    cosine = jnp.cos(angles)
    sine = jnp.sin(angles)
    first_half = values_in[..., :half_size]
    second_half = values_in[..., half_size:]
    return jnp.concatenate(
        [first_half * cosine - second_half * sine, second_half * cosine + first_half * sine],
        axis=-1,
    )


def attend(queries, key_rows, value_rows, visible):
    scores = jnp.einsum("bwhgd,bhld->bhgwl", queries, key_rows, preferred_element_type=jnp.float32)
    scores = score_cap * jnp.tanh(scores / score_cap)
    weights = jnp.where(visible[:, None, None], jnp.exp(scores), 0.0)
    weight_sum = jnp.sum(weights, axis=-1, keepdims=True)
    rounded = lax.optimization_barrier(weights.astype(jnp.bfloat16))
    summed = jnp.einsum(
        "bhgwl,bhld->bwhgd", rounded, value_rows, preferred_element_type=jnp.float32
    )
    return (summed / jnp.moveaxis(weight_sum, 3, 1)).astype(jnp.bfloat16)


def per_device(
    window_ids,
    pool_ids,
    accepted,
    converged,
    cache_lens,
    table,
    attn_gain,
    post_gain,
    final_gain,
    w_query,
    w_key,
    w_value,
    w_out,
    cache_keys,
    cache_values,
):
    iter_count, local_batch, width = window_ids.shape
    model_width = table.shape[1]
    vocab_rows = table.shape[0]
    head_size = cache_keys.shape[3]
    kv_local = cache_keys.shape[1]
    cache_slots = cache_keys.shape[2]
    local_rows = local_batch * width
    vocab_devices = lax.axis_size("vocab")
    batch_index = lax.axis_index("batch")
    vocab_index = lax.axis_index("vocab")
    all_windows, all_pools = (
        lax.all_gather(window_ids, "batch", axis=1, tiled=True),
        lax.all_gather(pool_ids, "batch", axis=1, tiled=True),
    )
    total_batch = all_windows.shape[1]
    first_id = (batch_index * vocab_devices + vocab_index) * vocab_rows
    ordered = jnp.transpose(all_windows, (1, 2, 0)) - first_id
    inside = (ordered >= 0) & (ordered < vocab_rows)
    looked_up = jnp.take(table, jnp.clip(ordered, 0, vocab_rows - 1), axis=0)
    lookup_terms = jnp.where(inside[..., None], looked_up.astype(jnp.float32), 0.0)
    column_rows = lax.psum_scatter(
        lookup_terms.astype(jnp.bfloat16), "batch", scatter_dimension=0, tiled=True
    )
    embedded_all = lax.psum(column_rows, "vocab").astype(jnp.float32)
    taken = jnp.where(converged == 1, width, accepted)
    offset = cache_lens
    slots = jnp.arange(width, dtype=jnp.int32)
    cache_visible = (
        jnp.arange(cache_slots, dtype=jnp.int32)[None, None, :] < cache_lens[:, None, None]
    )
    own_visible = slots[None, None, :] <= slots[None, :, None]
    key_list = [cache_keys]
    value_list = [cache_values]
    mask_list = [jnp.broadcast_to(cache_visible, (local_batch, width, cache_slots))]
    vocab_iota = jnp.arange(vocab_rows, dtype=jnp.int32)
    totals_out = []
    best_out = []
    score_out = []
    for step in range(iter_count):
        embedded = embedded_all[:, :, step] * math.sqrt(model_width)
        normed = (
            normalize(embedded, attn_gain).astype(jnp.bfloat16).reshape(local_rows, model_width)
        )
        positions = (offset[:, None] + slots[None, :])[:, :, None]
        queries = jnp.dot(normed, w_query, preferred_element_type=jnp.float32).reshape(
            local_batch, width, 2 * kv_local, head_size
        )
        queries = (
            (rotate(queries, positions) / math.sqrt(query_scalar))
            .astype(jnp.bfloat16)
            .reshape(local_batch, width, kv_local, 2, head_size)
        )
        keys_now = jnp.dot(normed, w_key, preferred_element_type=jnp.float32).reshape(
            local_batch, width, kv_local, head_size
        )
        keys_now = rotate(keys_now, positions).astype(jnp.bfloat16).transpose(0, 2, 1, 3)
        values_now = jnp.dot(normed, w_value, preferred_element_type=jnp.float32).reshape(
            local_batch, width, kv_local, head_size
        )
        values_now = values_now.astype(jnp.bfloat16).transpose(0, 2, 1, 3)
        all_keys = jnp.concatenate(key_list + [keys_now], axis=2)
        all_values = jnp.concatenate(value_list + [values_now], axis=2)
        visible = jnp.concatenate(
            mask_list + [jnp.broadcast_to(own_visible, (local_batch, width, width))], axis=2
        )
        attended = attend(queries, all_keys, all_values, visible).reshape(
            local_rows, 2 * kv_local * head_size
        )
        branch = jnp.dot(attended, w_out, preferred_element_type=jnp.float32)
        residual = embedded.reshape(local_rows, model_width)
        whole_branch = lax.psum(branch, "vocab")
        hidden = residual + normalize(whole_branch, post_gain)
        final_rows = normalize(hidden, final_gain).astype(jnp.bfloat16)
        pool_local = all_pools[step].reshape(total_batch * width) - first_id
        raw_logits = lax.dot_general(
            lax.all_gather(final_rows, "batch", axis=0, tiled=True),
            table,
            (((1,), (1,)), ((), ())),
            preferred_element_type=jnp.float32,
        )
        logits = logit_cap * jnp.tanh(raw_logits / logit_cap)
        exp_sums = jnp.sum(jnp.exp(logits), axis=-1)
        largest = jnp.max(logits, axis=-1)
        chosen = jnp.sum(
            jnp.where(vocab_iota[None, :] == pool_local[:, None], logits, 0.0), axis=-1
        )
        own_start = batch_index * local_rows
        sums_column, picks_column = (
            lax.psum_scatter(exp_sums, "batch", scatter_dimension=0, tiled=True),
            lax.psum_scatter(chosen, "batch", scatter_dimension=0, tiled=True),
        )
        sums_own, picks_own = lax.psum((sums_column, picks_column), "vocab")
        tops_joint = lax.pmax(largest, ("batch", "vocab"))
        tops_own = lax.dynamic_slice_in_dim(tops_joint, own_start, local_rows)
        log_sum = jnp.log(sums_own)
        totals_out.append(log_sum.reshape(local_batch, width))
        best_out.append(tops_own.reshape(local_batch, width))
        score_out.append((picks_own - log_sum).reshape(local_batch, width))
        if step + 1 < iter_count:
            key_list.append(keys_now)
            value_list.append(values_now)
            mask_list.append(
                jnp.broadcast_to(
                    slots[None, None, :] < taken[step][:, None, None], (local_batch, width, width)
                )
            )
            offset = offset + taken[step]
    return (jnp.stack(totals_out), jnp.stack(best_out), jnp.stack(score_out))


def solution(mesh):
    return jax.shard_map(
        per_device,
        mesh=mesh,
        in_specs=(
            P(None, "batch", None),
            P(None, "batch", None),
            P(None, "batch"),
            P(None, "batch"),
            P("batch"),
            P(("batch", "vocab"), None),
            P(),
            P(),
            P(),
            P(None, "vocab"),
            P(None, "vocab"),
            P(None, "vocab"),
            P("vocab", None),
            P("batch", "vocab", None, None),
            P("batch", "vocab", None, None),
        ),
        out_specs=(P(None, "batch", None), P(None, "batch", None), P(None, "batch", None)),
        check_vma=False,
    )
```

profile of v0, /device:TPU:10, one launch (start us, length us, event | category | flops | bytes accessed | tf_op | source)
XLA Modules:
  0.0 360.0 jit_solution(6029630634133774123)
XLA Ops:
  8.1 14.3 %all_gather.15 = s32[3,16,8]{2,0,1:T(4,128)S(1)} all-gather(s32[3,2,8]{2,0,1:T(4,128)S(1)} %copy.76), channel_id=1, replica_groups=mesh['batch'=8,'vocab'=4] {'batch'}, dimensions={1}, use_global_device_ids=true | all-gather | bytes 1728 | tf_op jit(solution)/shard_map/all_gather | solution.py:75
  22.8 12.2 %gather_fusion = bf16[384,4608]{1,0:T(8,128)(2,1)} fusion(bf16[512,4608]{1,0:T(8,128)(2,1)} %param.20, s32[1024]{0:T(1024)S(1)} %pad_clamp_fusion), kind=kCustom, calls=%fused_computation | custom fusion | bytes 7079424 | tf_op jit(solution)/shard_map/jit(_take)/gather | solution.py:82
  35.0 7.3 %reshape.718 = bf16[16,8,3,4608]{3,2,1,0:T(4,128)(2,1)} reshape(bf16[384,4608]{1,0:T(8,128)(2,1)} %gather_fusion) | data formatting | bytes 7077888 | tf_op jit(solution)/shard_map/jit(_take)/gather | solution.py:82
  42.4 6.3 %select_convert_fusion = bf16[16,8,3,4608]{3,1,2,0:T(8,128)(2,1)} fusion(bf16[16,8,3,4608]{3,2,1,0:T(4,128)(2,1)} %reshape.718, pred[16,8,3]{1,2,0:T(4,128)(4,1)S(1)} %copy.79, pred[16,8,3]{1,2,0:T(4,128)(4,1)S(1)} %copy.78), kind=kLoop, calls=%fused_computation.1 | loop fusion | flops 7077888 | bytes 7078656 | tf_op jit(solution)/shard_map/convert_element_type | solution.py:85
  48.8 4.3 %copy.102 = bf16[256,4608]{1,0:T(8,128)(2,1)} copy(bf16[256,4608]{0,1:T(8,128)(2,1)} %bitcast.314) | data formatting | bytes 4718592 | tf_op jit(solution)/shard_map/dot_general | solution.py:108
  53.7 36.1 %reduce-scatter.2.cloned.1.call-done = bf16[2,8,3,4608]{3,1,2,0:T(8,128)(2,1)} async-done(((bf16[16,8,3,4608]{3,1,2,0:T(8,128)(2,1)}), bf16[2,8,3,4608]{3,1,2,0:T(8,128)(2,1)}) %reduce-scatter.2.cloned.1.call-update) | async-done | bytes 442384 | tf_op jit(solution)/shard_map/reduce_scatter | solution.py:84
  89.8 1.8 copy.82
  92.1 47.6 %all-reduce.13.cloned.1.call-done = bf16[2,8,3,4608]{3,1,0,2:T(8,128)(2,1)} async-done(((bf16[2,8,3,4608]{3,1,0,2:T(8,128)(2,1)}), bf16[2,8,3,4608]{3,1,0,2:T(8,128)(2,1)}) %all-reduce.13.cloned.1.call-update) | async-done | bytes 442384 | tf_op jit(solution)/shard_map/psum | solution.py:87
  141.1 1.6 fusion.45
  142.7 1.7 fusion.48
  151.1 1.2 fusion.70
  152.4 1.2 fusion.69
  153.7 50.5 %all-reduce.15.cloned.1.call-done = (f32[16,4608]{1,0:T(8,128)}, f32[16,4608]{1,0:T(8,128)}, f32[16,4608]{1,0:T(8,128)}) async-done(((f32[16,4608]{1,0:T(8,128)}, f32[16,4608]{1,0:T(8,128)}, f32[16,4608]{1,0:T(8,128)}), (f32[16,4608]{1,0:T(8,128)}, f32[16,4608]{1,0:T(8,128)}, f32[16,4608]{1,0:T(8,128)})) %all-reduce.15.cloned.1.call-update) | async-done | bytes 884752 | tf_op jit(solution)/shard_map/psum | solution.py:134
  207.7 1.5 multiply_reduce_fusion.4
  211.5 14.2 %all_gather.19 = s32[3,16,8]{2,0,1:T(4,128)S(1)} all-gather(s32[3,2,8]{2,0,1:T(4,128)S(1)} %copy.92), channel_id=1, replica_groups=mesh['batch'=8,'vocab'=4] {'batch'}, dimensions={1}, use_global_device_ids=true | all-gather | bytes 1728 | tf_op jit(solution)/shard_map/all_gather | solution.py:76
  227.3 5.9 %all-gather.4.cloned.1.call-done = bf16[128,4608]{1,0:T(8,128)(2,1)} async-done(((bf16[16,4608]{1,0:T(8,128)(2,1)}), bf16[128,4608]{1,0:T(8,128)(2,1)}) %all-gather.4.cloned.1.call-update) | async-done | bytes 1179664 | tf_op jit(solution)/shard_map/all_gather | solution.py:139
  233.2 4.5 %select_reduce_fusion.2 = (f32[128]{0:T(128)S(1)}, f32[128]{0:T(128)S(1)}, f32[128]{0:T(128)S(1)}) fusion(s32[128]{0:T(128)S(1)} %sub.79, bf16[128,4608]{1,0:T(8,128)(2,1)} %all-gather.4.cloned.1.call-done, bf16[512,4608]{1,0:T(8,128)(2,1)} %param.20), kind=kOutput, calls=%fused_computation.103 | convolution fusion | flops 604438144 | bytes 5900288 | tf_op jit(solution)/shard_map/dot_general | solution.py:138
  237.7 19.4 %all-gather.6.cloned.1.call-done = bf16[128,4608]{1,0:T(8,128)(2,1)} async-done(((bf16[16,4608]{1,0:T(8,128)(2,1)}), bf16[128,4608]{1,0:T(8,128)(2,1)}) %all-gather.6.cloned.1.call-update) | async-done | bytes 1179664 | tf_op jit(solution)/shard_map/all_gather | solution.py:139
  257.1 4.5 %select_reduce_fusion.1 = (f32[128]{0:T(128)S(1)}, f32[128]{0:T(128)S(1)}, f32[128]{0:T(128)S(1)}) fusion(s32[128]{0:T(128)S(1)} %sub.82, bf16[128,4608]{1,0:T(8,128)(2,1)} %all-gather.6.cloned.1.call-done, bf16[512,4608]{1,0:T(8,128)(2,1)} %param.20), kind=kOutput, calls=%fused_computation.101 | convolution fusion | flops 604438144 | bytes 5900288 | tf_op jit(solution)/shard_map/dot_general | solution.py:138
  261.6 19.5 %all-gather.8.cloned.1.call-done = bf16[128,4608]{1,0:T(8,128)(2,1)} async-done(((bf16[16,4608]{1,0:T(8,128)(2,1)}), bf16[128,4608]{1,0:T(8,128)(2,1)}) %all-gather.8.cloned.1.call-update) | async-done | bytes 1179664 | tf_op jit(solution)/shard_map/all_gather | solution.py:139
  281.0 4.5 %select_reduce_fusion = (f32[128]{0:T(128)S(1)}, f32[128]{0:T(128)S(1)}, f32[128]{0:T(128)S(1)}) fusion(s32[128]{0:T(128)S(1)} %sub.85, bf16[128,4608]{1,0:T(8,128)(2,1)} %all-gather.8.cloned.1.call-done, bf16[512,4608]{1,0:T(8,128)(2,1)} %param.20), kind=kOutput, calls=%fused_computation.99 | convolution fusion | flops 604438144 | bytes 5900288 | tf_op jit(solution)/shard_map/dot_general | solution.py:138
  285.5 12.1 %all-reduce.7 = (f32[128]{0:T(128)S(1)}, f32[128]{0:T(128)S(1)}, f32[128]{0:T(128)S(1)}, f32[128]{0:T(128)S(1)}, f32[128]{0:T(128)S(1)}, /*index=5*/f32[128]{0:T(128)S(1)}) all-reduce(f32[128]{0:T(128)S(1)} %get-tuple-element.17, f32[128]{0:T(128)S(1)} %get-tuple-element.14, ...), channel_id=5, replica_groups=mesh['batch'=8,'vocab'=4] {'batch'}, use_global_device_ids=true, to_apply=%region_24.25.clone | all-reduce | flops 768 | bytes 6144
  298.1 8.0 %all-reduce.8 = (f32[16]{0:T(128)S(1)}, f32[16]{0:T(128)S(1)}, f32[16]{0:T(128)S(1)}, f32[16]{0:T(128)S(1)}, f32[16]{0:T(128)S(1)}, /*index=5*/f32[16]{0:T(128)S(1)}) all-reduce(f32[16]{0:T(128)S(1)} %dynamic-slice.5, f32[16]{0:T(128)S(1)} %dynamic-slice.3, f32[16]{0:T(128)S(1)} %dynamic-slice.1, ...), channel_id=1, replica_groups=mesh['batch'=8,'vocab'=4] {'vocab'}, use_global_device_ids=true, to_apply=%region_25.26 | all-reduce | flops 96 | bytes 768 | tf_op jit(solution)/shard_map/psum | solution.py:155
  306.4 44.3 %all-reduce.6 = (f32[128]{0:T(128)S(1)}, f32[128]{0:T(128)S(1)}, f32[128]{0:T(128)S(1)}) all-reduce(f32[128]{0:T(128)S(1)} %get-tuple-element.16, f32[128]{0:T(128)S(1)} %get-tuple-element.13, f32[128]{0:T(128)S(1)} %get-tuple-element.10), channel_id=1, replica_groups=mesh['batch'=8,'vocab'=4] {'batch','vocab'}, use_global_device_ids=true, to_apply=%region_31.32 | all-reduce | flops 384 | bytes 3072 | tf_op jit(solution)/shard_map/pmax | solution.py:156
  (131 shorter events, 20.4 us)
Async XLA Ops:
  7.2 142.7 %copy-start = (bf16[256,4608]{1,0:T(8,128)(2,1)S(1)}, bf16[256,4608]{1,0:T(8,128)(2,1)}, u32[]{:S(2)}) copy-start(bf16[256,4608]{1,0:T(8,128)(2,1)} %param.27) | copy-start | bytes 7077892
  7.2 82.6 %reduce-scatter.2.cloned.1.call-start = ((), (), s32[]{:S(2)}) async-start(), calls=%async_computation.1 | async-start | bytes 3981312 | tf_op jit(solution)/shard_map/reduce_scatter | solution.py:84
  48.7 90.9 %all-reduce.13.cloned.1.call-start = ((), (), s32[]{:S(2)}) async-start(), calls=%async_computation.2 | async-start | bytes 884736 | tf_op jit(solution)/shard_map/psum | solution.py:87
  48.8 4.4 %copy-start.14 = (s32[2]{0:T(128)S(1)}, s32[2]{0:T(128)}, u32[]{:S(2)}) copy-start(s32[2]{0:T(128)} %param.19) | copy-start | bytes 28
  48.8 4.5 %copy-start.12 = (s32[2,2]{1,0:T(2,128)S(1)}, s32[2,2]{1,0:T(2,128)}, u32[]{:S(2)}) copy-start(s32[2,2]{1,0:T(2,128)} %param.17) | copy-start | bytes 52
  48.8 4.5 %copy-start.13 = (s32[2,2]{1,0:T(2,128)S(1)}, s32[2,2]{1,0:T(2,128)}, u32[]{:S(2)}) copy-start(s32[2,2]{1,0:T(2,128)} %param.18) | copy-start | bytes 52
  53.2 87.9 %copy-start.4 = (f32[4608]{0:T(1024)S(1)}, f32[4608]{0:T(1024)}, u32[]{:S(2)}) copy-start(f32[4608]{0:T(1024)} %param.21) | copy-start | bytes 55300
  91.6 112.6 %all-reduce.15.cloned.1.call-start = ((), (), s32[]{:S(2)}) async-start(), calls=%async_computation.6 | async-start | bytes 1769472 | tf_op jit(solution)/shard_map/psum | solution.py:134
  139.7 4.7 %copy-start.3 = (bf16[4608,128]{1,0:T(8,128)(2,1)S(1)}, bf16[4608,128]{1,0:T(8,128)(2,1)}, u32[]{:S(2)}) copy-start(bf16[4608,128]{1,0:T(8,128)(2,1)} %param.26) | copy-start | bytes 3538948
  142.6 2.4 copy-start.2
  144.7 1.7 copy-start.1
  147.1 1.7 copy-start.15
  147.8 2.1 copy-start.8
  152.4 55.3 %copy-start.9 = (f32[4608]{0:T(1024)S(1)}, f32[4608]{0:T(1024)}, u32[]{:S(2)}) copy-start(f32[4608]{0:T(1024)} %param.22) | copy-start | bytes 55300
  153.6 55.6 %copy-start.10 = (f32[4608]{0:T(1024)S(1)}, f32[4608]{0:T(1024)}, u32[]{:S(2)}) copy-start(f32[4608]{0:T(1024)} %param.23) | copy-start | bytes 55300
  153.6 79.6 %all-gather.4.cloned.1.call-start = ((), (), s32[]{:S(2)}) async-start(), calls=%async_computation.3 | async-start | bytes 1327104 | tf_op jit(solution)/shard_map/all_gather | solution.py:139
  204.2 5.1 %copy-start.5 = (f32[16,4608]{1,0:T(8,128)S(1)}, f32[16,4608]{1,0:T(8,128)}, u32[]{:S(2)}) copy-start(f32[16,4608]{1,0:T(8,128)} %get-tuple-element.36) | copy-start | bytes 884740
  204.2 5.1 %copy-start.6 = (f32[16,4608]{1,0:T(8,128)S(1)}, f32[16,4608]{1,0:T(8,128)}, u32[]{:S(2)}) copy-start(f32[16,4608]{1,0:T(8,128)} %get-tuple-element.37) | copy-start | bytes 884740
  204.2 5.1 %copy-start.7 = (f32[16,4608]{1,0:T(8,128)S(1)}, f32[16,4608]{1,0:T(8,128)}, u32[]{:S(2)}) copy-start(f32[16,4608]{1,0:T(8,128)} %get-tuple-element.38) | copy-start | bytes 884740
  206.5 4.9 %copy-start.11 = (s32[3,2,8]{2,1,0:T(2,128)S(1)}, s32[3,2,8]{2,1,0:T(2,128)}, u32[]{:S(2)}) copy-start(s32[3,2,8]{2,1,0:T(2,128)} %param.16) | copy-start | bytes 580
  207.6 18.4 %copy-start.16 = (u32[32]{0:T(128)S(1)}, u32[32]{0:T(128)}, u32[]{:S(2)}) copy-start(u32[32]{0:T(128)} %constant.94) | copy-start | bytes 388
  210.3 46.8 %all-gather.6.cloned.1.call-start = ((), (), s32[]{:S(2)}) async-start(), calls=%async_computation.4 | async-start | bytes 1327104 | tf_op jit(solution)/shard_map/all_gather | solution.py:139
  210.9 70.2 %all-gather.8.cloned.1.call-start = ((), (), s32[]{:S(2)}) async-start(), calls=%async_computation.5 | async-start | bytes 1327104 | tf_op jit(solution)/shard_map/all_gather | solution.py:139
Sparse Core Ops, SparseCore 0:
  48.9 40.8 reduce-scatter.1
  92.8 46.8 all-reduce.12
  153.7 50.3 all-reduce.14
  210.4 22.7 all-gather.3
  234.7 22.3 all-gather.5
  258.6 22.4 all-gather.7
where the time goes:
time: 361 us; the launch traced here: 360 us
  waiting for transfers between devices  180 us (50%)
  blocking collectives  92.9 us (26%)
  local copies, waits for them, and re-layouts  30 us (8%)
  matrix products  24.9 us (7%)
  other arithmetic  16.6 us (5%)
  between operations  15.1 us (4%)
    psum x1, waiting for transfers between devices, per_device(): whole_branch = lax.psum(branch, 'vocab')  50.5 us
    psum x1, waiting for transfers between devices, per_device(): embedded_all = lax.psum(column_rows, 'vocab').astype(jnp.float32)  47.6 us
    all_gather x3, waiting for transfers between devices, per_device(): lax.all_gather(final_rows, 'batch', axis=0, tiled=True)  44.7 us
    pmax x1, blocking collectives, per_device(): tops_joint = lax.pmax(largest, ('batch', 'vocab'))  44.3 us
    reduce_scatter x1, waiting for transfers between devices, per_device(): lax.psum_scatter(lookup_terms.astype(jnp.bfloat16), 'batch', scatter_dime...  36.1 us
    gather x2, local copies, waits for them, and re-layouts, per_device(): looked_up = jnp.take(table, jnp.clip(ordered, 0, vocab_rows - 1), axis=0)  19.4 us
    all_gather x1, blocking collectives, per_device(): lax.all_gather(window_ids, 'batch', axis=1, tiled=True)  14.3 us
    all_gather x1, blocking collectives, per_device(): lax.all_gather(pool_ids, 'batch', axis=1, tiled=True)  14.2 us
  transfers between devices with their start and end apart: 6, of which 6 were waited for; matrix products, arithmetic and copies ran while one was open for 4% of the time, Pallas kernels for 0%

commit v1 on v0

--- a/solution.py
+++ b/solution.py
@@ -61,6 +61,11 @@
     cache_keys,
     cache_values,
 ):
+
+    def manage_steps_all(chunk, net_axis="vocab"):
+        then = jnp.sum(lax.all_gather(chunk, axis_name=net_axis), axis=0)
+        return then
+
     iter_count, local_batch, width = window_ids.shape
     model_width = table.shape[1]
     vocab_rows = table.shape[0]
@@ -84,7 +89,7 @@
     column_rows = lax.psum_scatter(
         lookup_terms.astype(jnp.bfloat16), "batch", scatter_dimension=0, tiled=True
     )
-    embedded_all = lax.psum(column_rows, "vocab").astype(jnp.float32)
+    embedded_all = manage_steps_all(column_rows).astype(jnp.float32)
     taken = jnp.where(converged == 1, width, accepted)
     offset = cache_lens
     slots = jnp.arange(width, dtype=jnp.int32)

time: 361 us -> 347 us (0.961)
  waiting for transfers between devices: 180 us -> 168 us
    psum x1 -> x0, waiting for transfers between devices: 47.6 us -> none  [per_device(): embedded_all = lax.psum(column_rows, 'vocab').astype(jnp.float32)]
    all_gather x0 -> x1, waiting for transfers between devices: none -> 31.2 us  [manage_steps_all(): then = jnp.sum(lax.all_gather(chunk, axis_name=net_axis), axis=0)]
    reduce_scatter x1, waiting for transfers between devices: 36.1 us -> 41 us  [per_device(): lax.psum_scatter(lookup_terms.astype(jnp.bfloat16), 'batch', scatter_dime...]
where the time goes in v1:
time: 347 us
  waiting for transfers between devices  168 us (48%)
  blocking collectives  92.9 us (27%)
  local copies, waits for them, and re-layouts  29 us (8%)
  matrix products  22.1 us (6%)
  other arithmetic  18.6 us (5%)
  between operations  15.1 us (4%)
    psum x1, waiting for transfers between devices, per_device(): whole_branch = lax.psum(branch, 'vocab')  50.4 us
    all_gather x3, waiting for transfers between devices, per_device(): lax.all_gather(final_rows, 'batch', axis=0, tiled=True)  44.7 us
    pmax x1, blocking collectives, per_device(): tops_joint = lax.pmax(largest, ('batch', 'vocab'))  44.3 us
    reduce_scatter x1, waiting for transfers between devices, per_device(): lax.psum_scatter(lookup_terms.astype(jnp.bfloat16), 'batch', scatter_dime...  41 us
    all_gather x1, waiting for transfers between devices, manage_steps_all(): then = jnp.sum(lax.all_gather(chunk, axis_name=net_axis), axis=0)  31.2 us
    gather x2, local copies, waits for them, and re-layouts, per_device(): looked_up = jnp.take(table, jnp.clip(ordered, 0, vocab_rows - 1), axis=0)  19.4 us
    all_gather x1, blocking collectives, per_device(): lax.all_gather(window_ids, 'batch', axis=1, tiled=True)  14.3 us
    all_gather x1, blocking collectives, per_device(): lax.all_gather(pool_ids, 'batch', axis=1, tiled=True)  14.2 us
  transfers between devices with their start and end apart: 6, of which 6 were waited for; matrix products, arithmetic and copies ran while one was open for 4% of the time, Pallas kernels for 0%

profile of v1, /device:TPU:10, one launch (start us, length us, event | category | flops | bytes accessed | tf_op | source)
XLA Modules:
  0.0 346.6 jit_solution(12664887982420587214)
XLA Ops:
  8.1 14.3 %all_gather.21 = s32[3,16,8]{2,0,1:T(4,128)S(1)} all-gather(s32[3,2,8]{2,0,1:T(4,128)S(1)} %copy.81), channel_id=1, replica_groups=mesh['batch'=8,'vocab'=4] {'batch'}, dimensions={1}, use_global_device_ids=true | all-gather | bytes 1728 | tf_op jit(solution)/shard_map/all_gather | solution.py:80
  22.8 12.2 %gather_fusion = bf16[384,4608]{1,0:T(8,128)(2,1)} fusion(bf16[512,4608]{1,0:T(8,128)(2,1)} %param.20, s32[1024]{0:T(1024)S(1)} %pad_clamp_fusion), kind=kCustom, calls=%fused_computation | custom fusion | bytes 7079424 | tf_op jit(solution)/shard_map/jit(_take)/gather | solution.py:87
  35.0 7.3 %reshape.718 = bf16[16,8,3,4608]{3,2,1,0:T(4,128)(2,1)} reshape(bf16[384,4608]{1,0:T(8,128)(2,1)} %gather_fusion) | data formatting | bytes 7077888 | tf_op jit(solution)/shard_map/jit(_take)/gather | solution.py:87
  42.4 6.3 %select_convert_fusion = bf16[16,8,3,4608]{3,1,2,0:T(8,128)(2,1)} fusion(bf16[16,8,3,4608]{3,2,1,0:T(4,128)(2,1)} %reshape.718, pred[16,8,3]{1,2,0:T(4,128)(4,1)S(1)} %copy.84, pred[16,8,3]{1,2,0:T(4,128)(4,1)S(1)} %copy.83), kind=kLoop, calls=%fused_computation.1 | loop fusion | flops 7077888 | bytes 7078656 | tf_op jit(solution)/shard_map/convert_element_type | solution.py:90
  48.8 41.0 %reduce-scatter.2.cloned.1.call-done = bf16[2,8,3,4608]{3,1,2,0:T(8,128)(2,1)} async-done(((bf16[16,8,3,4608]{3,1,2,0:T(8,128)(2,1)}), bf16[2,8,3,4608]{3,1,2,0:T(8,128)(2,1)}) %reduce-scatter.2.cloned.1.call-update) | async-done | bytes 442384 | tf_op jit(solution)/shard_map/reduce_scatter | solution.py:89
  90.1 4.3 %copy.111 = bf16[256,4608]{1,0:T(8,128)(2,1)} copy(bf16[256,4608]{0,1:T(8,128)(2,1)} %bitcast.315) | data formatting | bytes 4718592 | tf_op jit(solution)/shard_map/dot_general | solution.py:113
  95.2 31.2 %all-gather.12.cloned.1.call-done = bf16[8,8,3,4608]{3,1,2,0:T(8,128)(2,1)} async-done(((bf16[2,8,3,4608]{3,1,2,0:T(8,128)(2,1)}), bf16[8,8,3,4608]{3,1,2,0:T(8,128)(2,1)}) %all-gather.12.cloned.1.call-update) | async-done | bytes 1769488 | tf_op jit(solution)/shard_map/all_gather | solution.py:66
  126.4 1.8 reduce_sum.174
  136.6 1.2 fusion.71
  137.9 1.2 fusion.70
  139.1 1.2 fusion.69
  140.4 50.4 %all-reduce.12.cloned.1.call-done = (f32[16,4608]{1,0:T(8,128)}, f32[16,4608]{1,0:T(8,128)}, f32[16,4608]{1,0:T(8,128)}) async-done(((f32[16,4608]{1,0:T(8,128)}, f32[16,4608]{1,0:T(8,128)}, f32[16,4608]{1,0:T(8,128)}), (f32[16,4608]{1,0:T(8,128)}, f32[16,4608]{1,0:T(8,128)}, f32[16,4608]{1,0:T(8,128)})) %all-reduce.12.cloned.1.call-update) | async-done | bytes 884752 | tf_op jit(solution)/shard_map/psum | solution.py:139
  190.8 1.2 multiply_reduce_fusion.1
  194.3 1.5 multiply_reduce_fusion.4
  198.1 14.2 %all_gather.27 = s32[3,16,8]{2,0,1:T(4,128)S(1)} all-gather(s32[3,2,8]{2,0,1:T(4,128)S(1)} %copy.101), channel_id=1, replica_groups=mesh['batch'=8,'vocab'=4] {'batch'}, dimensions={1}, use_global_device_ids=true | all-gather | bytes 1728 | tf_op jit(solution)/shard_map/all_gather | solution.py:81
  214.0 5.9 %all-gather.6.cloned.1.call-done = bf16[128,4608]{1,0:T(8,128)(2,1)} async-done(((bf16[16,4608]{1,0:T(8,128)(2,1)}), bf16[128,4608]{1,0:T(8,128)(2,1)}) %all-gather.6.cloned.1.call-update) | async-done | bytes 1179664 | tf_op jit(solution)/shard_map/all_gather | solution.py:144
  219.8 4.5 %select_reduce_fusion.2 = (f32[128]{0:T(128)S(1)}, f32[128]{0:T(128)S(1)}, f32[128]{0:T(128)S(1)}) fusion(s32[128]{0:T(128)S(1)} %sub.79, bf16[128,4608]{1,0:T(8,128)(2,1)} %all-gather.6.cloned.1.call-done, bf16[512,4608]{1,0:T(8,128)(2,1)} %param.20), kind=kOutput, calls=%fused_computation.106 | convolution fusion | flops 604438144 | bytes 5900288 | tf_op jit(solution)/shard_map/dot_general | solution.py:143
  224.3 19.4 %all-gather.8.cloned.1.call-done = bf16[128,4608]{1,0:T(8,128)(2,1)} async-done(((bf16[16,4608]{1,0:T(8,128)(2,1)}), bf16[128,4608]{1,0:T(8,128)(2,1)}) %all-gather.8.cloned.1.call-update) | async-done | bytes 1179664 | tf_op jit(solution)/shard_map/all_gather | solution.py:144
  243.7 4.5 %select_reduce_fusion.1 = (f32[128]{0:T(128)S(1)}, f32[128]{0:T(128)S(1)}, f32[128]{0:T(128)S(1)}) fusion(s32[128]{0:T(128)S(1)} %sub.82, bf16[128,4608]{1,0:T(8,128)(2,1)} %all-gather.8.cloned.1.call-done, bf16[512,4608]{1,0:T(8,128)(2,1)} %param.20), kind=kOutput, calls=%fused_computation.104 | convolution fusion | flops 604438144 | bytes 5900288 | tf_op jit(solution)/shard_map/dot_general | solution.py:143
  248.2 19.5 %all-gather.10.cloned.1.call-done = bf16[128,4608]{1,0:T(8,128)(2,1)} async-done(((bf16[16,4608]{1,0:T(8,128)(2,1)}), bf16[128,4608]{1,0:T(8,128)(2,1)}) %all-gather.10.cloned.1.call-update) | async-done | bytes 1179664 | tf_op jit(solution)/shard_map/all_gather | solution.py:144
  267.7 4.5 %select_reduce_fusion = (f32[128]{0:T(128)S(1)}, f32[128]{0:T(128)S(1)}, f32[128]{0:T(128)S(1)}) fusion(s32[128]{0:T(128)S(1)} %sub.85, bf16[128,4608]{1,0:T(8,128)(2,1)} %all-gather.10.cloned.1.call-done, bf16[512,4608]{1,0:T(8,128)(2,1)} %param.20), kind=kOutput, calls=%fused_computation.102 | convolution fusion | flops 604438144 | bytes 5900288 | tf_op jit(solution)/shard_map/dot_general | solution.py:143
  272.2 12.1 %all-reduce.7 = (f32[128]{0:T(128)S(1)}, f32[128]{0:T(128)S(1)}, f32[128]{0:T(128)S(1)}, f32[128]{0:T(128)S(1)}, f32[128]{0:T(128)S(1)}, /*index=5*/f32[128]{0:T(128)S(1)}) all-reduce(f32[128]{0:T(128)S(1)} %get-tuple-element.11, f32[128]{0:T(128)S(1)} %get-tuple-element.8, ...), channel_id=6, replica_groups=mesh['batch'=8,'vocab'=4] {'batch'}, use_global_device_ids=true, to_apply=%region_24.25.clone | all-reduce | flops 768 | bytes 6144
  284.7 8.0 %all-reduce.8 = (f32[16]{0:T(128)S(1)}, f32[16]{0:T(128)S(1)}, f32[16]{0:T(128)S(1)}, f32[16]{0:T(128)S(1)}, f32[16]{0:T(128)S(1)}, /*index=5*/f32[16]{0:T(128)S(1)}) all-reduce(f32[16]{0:T(128)S(1)} %dynamic-slice.5, f32[16]{0:T(128)S(1)} %dynamic-slice.3, f32[16]{0:T(128)S(1)} %dynamic-slice.1, ...), channel_id=1, replica_groups=mesh['batch'=8,'vocab'=4] {'vocab'}, use_global_device_ids=true, to_apply=%region_25.26 | all-reduce | flops 96 | bytes 768 | tf_op jit(solution)/shard_map/psum | solution.py:160
  293.0 44.3 %all-reduce.6 = (f32[128]{0:T(128)S(1)}, f32[128]{0:T(128)S(1)}, f32[128]{0:T(128)S(1)}) all-reduce(f32[128]{0:T(128)S(1)} %get-tuple-element.10, f32[128]{0:T(128)S(1)} %get-tuple-element.7, f32[128]{0:T(128)S(1)} %get-tuple-element.4), channel_id=1, replica_groups=mesh['batch'=8,'vocab'=4] {'batch','vocab'}, use_global_device_ids=true, to_apply=%region_31.32 | all-reduce | flops 384 | bytes 3072 | tf_op jit(solution)/shard_map/pmax | solution.py:161
  (135 shorter events, 19.5 us)
Async XLA Ops:
  7.2 129.4 %copy-start = (bf16[256,4608]{1,0:T(8,128)(2,1)S(1)}, bf16[256,4608]{1,0:T(8,128)(2,1)}, u32[]{:S(2)}) copy-start(bf16[256,4608]{1,0:T(8,128)(2,1)} %param.27) | copy-start | bytes 7077892
  7.2 82.6 %reduce-scatter.2.cloned.1.call-start = ((), (), s32[]{:S(2)}) async-start(), calls=%async_computation.1 | async-start | bytes 3981312 | tf_op jit(solution)/shard_map/reduce_scatter | solution.py:89
  48.7 77.7 %all-gather.12.cloned.1.call-start = ((), (), s32[]{:S(2)}) async-start(), calls=%async_computation.5 | async-start | bytes 2211840 | tf_op jit(solution)/shard_map/all_gather | solution.py:66
  89.8 101.0 %all-reduce.12.cloned.1.call-start = ((), (), s32[]{:S(2)}) async-start(), calls=%async_computation.6 | async-start | bytes 1769472 | tf_op jit(solution)/shard_map/psum | solution.py:139
  90.0 4.4 %copy-start.14 = (s32[2]{0:T(128)S(1)}, s32[2]{0:T(128)}, u32[]{:S(2)}) copy-start(s32[2]{0:T(128)} %param.19) | copy-start | bytes 28
  90.0 4.5 %copy-start.12 = (s32[2,2]{1,0:T(2,128)S(1)}, s32[2,2]{1,0:T(2,128)}, u32[]{:S(2)}) copy-start(s32[2,2]{1,0:T(2,128)} %param.17) | copy-start | bytes 52
  90.1 4.5 %copy-start.13 = (s32[2,2]{1,0:T(2,128)S(1)}, s32[2,2]{1,0:T(2,128)}, u32[]{:S(2)}) copy-start(s32[2,2]{1,0:T(2,128)} %param.18) | copy-start | bytes 52
  126.4 2.8 copy-start.7
  128.2 2.0 copy-start.2
  130.2 1.3 copy-start.3
  131.5 1.7 copy-start.1
  133.8 1.7 copy-start.15
  134.5 2.1 copy-start.8
  139.1 55.2 %copy-start.9 = (f32[4608]{0:T(1024)S(1)}, f32[4608]{0:T(1024)}, u32[]{:S(2)}) copy-start(f32[4608]{0:T(1024)} %param.22) | copy-start | bytes 55300
  140.3 55.5 %copy-start.10 = (f32[4608]{0:T(1024)S(1)}, f32[4608]{0:T(1024)}, u32[]{:S(2)}) copy-start(f32[4608]{0:T(1024)} %param.23) | copy-start | bytes 55300
  140.4 79.5 %all-gather.6.cloned.1.call-start = ((), (), s32[]{:S(2)}) async-start(), calls=%async_computation.2 | async-start | bytes 1327104 | tf_op jit(solution)/shard_map/all_gather | solution.py:144
  190.8 5.1 %copy-start.4 = (f32[16,4608]{1,0:T(8,128)S(1)}, f32[16,4608]{1,0:T(8,128)}, u32[]{:S(2)}) copy-start(f32[16,4608]{1,0:T(8,128)} %get-tuple-element.33) | copy-start | bytes 884740
  190.8 5.1 %copy-start.5 = (f32[16,4608]{1,0:T(8,128)S(1)}, f32[16,4608]{1,0:T(8,128)}, u32[]{:S(2)}) copy-start(f32[16,4608]{1,0:T(8,128)} %get-tuple-element.34) | copy-start | bytes 884740
  190.8 5.1 %copy-start.6 = (f32[16,4608]{1,0:T(8,128)S(1)}, f32[16,4608]{1,0:T(8,128)}, u32[]{:S(2)}) copy-start(f32[16,4608]{1,0:T(8,128)} %get-tuple-element.35) | copy-start | bytes 884740
  193.2 4.9 %copy-start.11 = (s32[3,2,8]{2,1,0:T(2,128)S(1)}, s32[3,2,8]{2,1,0:T(2,128)}, u32[]{:S(2)}) copy-start(s32[3,2,8]{2,1,0:T(2,128)} %param.16) | copy-start | bytes 580
  194.3 18.4 %copy-start.16 = (u32[32]{0:T(128)S(1)}, u32[32]{0:T(128)}, u32[]{:S(2)}) copy-start(u32[32]{0:T(128)} %constant.96) | copy-start | bytes 388
  196.9 46.8 %all-gather.8.cloned.1.call-start = ((), (), s32[]{:S(2)}) async-start(), calls=%async_computation.3 | async-start | bytes 1327104 | tf_op jit(solution)/shard_map/all_gather | solution.py:144
  197.5 70.2 %all-gather.10.cloned.1.call-start = ((), (), s32[]{:S(2)}) async-start(), calls=%async_computation.4 | async-start | bytes 1327104 | tf_op jit(solution)/shard_map/all_gather | solution.py:144
Sparse Core Ops, SparseCore 0:
  48.9 40.8 reduce-scatter.1
  91.6 34.7 all-gather.11
  140.5 50.3 all-reduce.11
  197.0 22.7 all-gather.5
  221.3 22.3 all-gather.7
  245.2 22.4 all-gather.9
